TPU v7x, 32 devices: a whole 2x2x4 slice. The times are simulated.
32 devices in a mesh: fsdp: 4 (over z), model: 4 (over x, core), shift: 2 (over y).
Axes of the slice: x: 2, y: 2, z: 4, core: 2. Of those that a mesh axis runs over, the one named last changes fastest.
Arguments:
- w_query: float32 [9216, 4096], P(('shift', 'fsdp'), 'model'), parts along dimension 0, may hold values from -0.125 to 0.125
- first_query: float32 [9216, 4096], P(('shift', 'fsdp'), 'model'), parts along dimension 0, may hold values from -0.09375 to 0.09375
- second_query: float32 [9216, 4096], P(('shift', 'fsdp'), 'model'), parts along dimension 0, may hold values from -0.09375 to 0.09375
- w_key: float32 [9216, 2048], P(('shift', 'fsdp'), 'model'), parts along dimension 0, may hold values from -0.125 to 0.125
- first_key: float32 [9216, 2048], P(('shift', 'fsdp'), 'model'), parts along dimension 0, may hold values from -0.09375 to 0.09375
- second_key: float32 [9216, 2048], P(('shift', 'fsdp'), 'model'), parts along dimension 0, may hold values from -0.09375 to 0.09375
- w_value: float32 [9216, 2048], P(('shift', 'fsdp'), 'model'), parts along dimension 0, may hold values from -0.125 to 0.125
- first_value: float32 [9216, 2048], P(('shift', 'fsdp'), 'model'), parts along dimension 0, may hold values from -0.09375 to 0.09375
- second_value: float32 [9216, 2048], P(('shift', 'fsdp'), 'model'), parts along dimension 0, may hold values from -0.09375 to 0.09375
- norm_gain: float32 [9216], P(('shift', 'fsdp')), parts along dimension 0, may hold values from 0.25 to 1.75
Outputs:
- ready_query: bfloat16 [9216, 4096], P('shift', 'model'), parts along dimension 0
- ready_key: bfloat16 [9216, 2048], P('shift', 'model'), parts along dimension 0
- ready_value: bfloat16 [9216, 2048], P('shift', 'model'), parts along dimension 0
- scale_query: float32 [8192], P(('shift', 'model')), parts along dimension 0
- scale_key: float32 [4096], P(('shift', 'model')), parts along dimension 0
- scale_value: float32 [4096], P(('shift', 'model')), parts along dimension 0
There are 2 independent parts, one for each index of `shift`. A program takes and returns all parts, laid end to end along the dimension named above; each array names one. Nothing has to cross between parts.
All inputs are finite; a program needn't handle non-finite values. Where the computation divides by a largest or mean magnitude, that divisor is 1e-20 or more.
Results may differ from a plain program's by a relative error of at most 0.001.
Values may be sent and summed in bfloat16 or wider, within the bound.
A program may use at most 128 MiB of HBM per device.

v0:
```python
import jax
import jax.numpy as jnp
from jax import lax
from jax.sharding import PartitionSpec as P

learn_rate = 0.2
hold_rate = 0.8


def body(
    w_query,
    first_query,
    second_query,
    w_key,
    first_key,
    second_key,
    w_value,
    first_value,
    second_value,
    norm_gain,
):
    hold_query = hold_rate * first_query + second_query
    latest_query = w_query - learn_rate * hold_query
    hold_key = hold_rate * first_key + second_key
    latest_key = w_key - learn_rate * hold_key
    hold_value = hold_rate * first_value + second_value
    latest_value = w_value - learn_rate * hold_value
    latest_gained_query = latest_query * norm_gain[:, None]
    latest_gained_key = latest_key * norm_gain[:, None]
    latest_gained_value = latest_value * norm_gain[:, None]
    scale_query, scale_key, scale_value = lax.pmax(
        (
            jnp.max(jnp.abs(latest_gained_query), axis=0),
            jnp.max(jnp.abs(latest_gained_key), axis=0),
            jnp.max(jnp.abs(latest_gained_value), axis=0),
        ),
        "fsdp",
    )
    narrow_query, narrow_key, narrow_value = (
        (latest_gained_query / scale_query).astype(jnp.bfloat16),
        (latest_gained_key / scale_key).astype(jnp.bfloat16),
        (latest_gained_value / scale_value).astype(jnp.bfloat16),
    )
    ready_query, ready_key, ready_value = (
        lax.all_gather(narrow_query, "fsdp", axis=0, tiled=True),
        lax.all_gather(narrow_key, "fsdp", axis=0, tiled=True),
        lax.all_gather(narrow_value, "fsdp", axis=0, tiled=True),
    )
    return (ready_query, ready_key, ready_value, scale_query, scale_key, scale_value)


def solution(mesh):
    placed = (
        P(("shift", "fsdp"), "model"),
        P(("shift", "fsdp"), "model"),
        P(("shift", "fsdp"), "model"),
        P(("shift", "fsdp"), "model"),
        P(("shift", "fsdp"), "model"),
        P(("shift", "fsdp"), "model"),
        P(("shift", "fsdp"), "model"),
        P(("shift", "fsdp"), "model"),
        P(("shift", "fsdp"), "model"),
        P(("shift", "fsdp")),
    )
    return jax.shard_map(
        body,
        mesh=mesh,
        in_specs=placed,
        out_specs=(
            P("shift", "model"),
            P("shift", "model"),
            P("shift", "model"),
            P(("shift", "model")),
            P(("shift", "model")),
            P(("shift", "model")),
        ),
        check_vma=False,
    )
```

profile of v0, /device:TPU:0, one launch (start us, length us, event | category | flops | bytes accessed | tf_op | source)
XLA Modules:
  0.0 404.1 jit_solution(4001969598912687606)
XLA Ops:
  7.2 0.0 copy-start.7
  7.2 0.0 all-gather.6.cloned.1.call-start
  7.2 0.0 copy-start.1
  7.2 0.0 copy-start.2
  7.2 0.0 copy-start.3
  7.3 0.0 copy-start.4
  7.3 0.0 copy-start.5
  7.3 0.0 copy-start.6
  7.3 8.6 %abs_reduce_fusion = (f32[1024]{0:T(1024)S(1)}, f32[1152,1024]{1,0:T(8,128)}) fusion(f32[1152]{0:T(1024)} %param.19, f32[1152,1024]{1,0:T(8,128)} %param.10, f32[1152,1024]{1,0:T(8,128)} %param.12, f32[1152,1024]{1,0:T(8,128)} %param.11), kind=kLoop, calls=%fused_computation.1 | loop fusion | flops 8256512 | bytes 18883072 | tf_op jit(solution)/shard_map/reduce_max | solution.py:33
  15.9 0.0 copy-done.7
  15.9 0.8 copy-done.4
  16.7 0.8 copy-done.5
  17.5 0.7 copy-done.6
  18.2 2.4 abs_reduce_fusion.1
  20.6 13.7 %all-reduce = (f32[1024]{0:T(1024)S(1)}, f32[512]{0:T(512)S(1)}, f32[512]{0:T(512)S(1)}) all-reduce(f32[1024]{0:T(1024)S(1)} %get-tuple-element.13, f32[512]{0:T(512)S(1)} %get-tuple-element.15, f32[512]{0:T(512)S(1)} %get-tuple-element.9), channel_id=1, replica_groups=mesh['fsdp'=4,'model'=4,'shift'=2] {'fsdp'}, use_global_device_ids=true, to_apply=%region_1.0 | all-reduce | flops 2048 | bytes 16384 | tf_op jit(solution)/shard_map/pmax | solution.py:31
  34.3 0.0 copy-start.9
  34.3 0.0 copy-start.10
  34.3 0.0 copy-start.8
  34.3 3.0 divide_convert_fusion.2
  37.3 0.0 all-gather.6.cloned.1.call-update
  37.4 0.0 all-gather.8.cloned.1.call-start
  37.4 1.3 divide_convert_fusion.1
  38.7 0.0 all-gather.8.cloned.1.call-update
  38.8 0.0 all-gather.4.cloned.1.call-start
  38.8 4.4 %divide_convert_fusion = bf16[1152,1024]{1,0:T(8,128)(2,1)} fusion(f32[1152,1024]{1,0:T(8,128)} %get-tuple-element.14, f32[1024]{0:T(1024)S(1)} %get-tuple-element.26), kind=kLoop, calls=%fused_computation | loop fusion | flops 2359296 | bytes 7081984 | tf_op jit(solution)/shard_map/convert_element_type | solution.py:40
  43.3 0.0 all-gather.4.cloned.1.call-update
  43.3 81.8 %all-gather.6.cloned.1.call-done = bf16[4608,512]{1,0:T(8,128)(2,1)} async-done(((bf16[1152,512]{1,0:T(8,128)(2,1)}), bf16[4608,512]{1,0:T(8,128)(2,1)}) %all-gather.6.cloned.1.call-update) | async-done | bytes 4718608 | tf_op jit(solution)/shard_map/all_gather | solution.py:46
  125.1 89.4 %all-gather.8.cloned.1.call-done = bf16[4608,512]{1,0:T(8,128)(2,1)} async-done(((bf16[1152,512]{1,0:T(8,128)(2,1)}), bf16[4608,512]{1,0:T(8,128)(2,1)}) %all-gather.8.cloned.1.call-update) | async-done | bytes 4718608 | tf_op jit(solution)/shard_map/all_gather | solution.py:47
  214.5 167.3 %all-gather.4.cloned.1.call-done = bf16[4608,1024]{1,0:T(8,128)(2,1)} async-done(((bf16[1152,1024]{1,0:T(8,128)(2,1)}), bf16[4608,1024]{1,0:T(8,128)(2,1)}) %all-gather.4.cloned.1.call-update) | async-done | bytes 9437200 | tf_op jit(solution)/shard_map/all_gather | solution.py:45
  381.9 8.5 %copy.19 = bf16[4608,1024]{1,0:T(8,128)(2,1)} copy(bf16[4608,1024]{1,0:T(8,128)(2,1)} %all-gather.4.cloned.1.call-done) | data formatting | bytes 18874368
  390.4 5.0 %copy.20 = bf16[4608,512]{1,0:T(8,128)(2,1)} copy(bf16[4608,512]{1,0:T(8,128)(2,1)} %all-gather.6.cloned.1.call-done) | data formatting | bytes 9437184
  395.4 2.2 copy.21
  (8 shorter events, 0.0 us)
Async XLA Ops:
  7.2 8.7 %copy-start.7 = (f32[1152]{0:T(1024)S(1)}, f32[1152]{0:T(1024)}, u32[]{:S(2)}) copy-start(f32[1152]{0:T(1024)} %param.19) | copy-start | bytes 13828
  7.2 117.9 %all-gather.6.cloned.1.call-start = ((), (), s32[]{:S(2)}) async-start(), calls=%async_computation.1 | async-start | bytes 5898240 | tf_op jit(solution)/shard_map/all_gather | solution.py:46
  7.2 8.7 %copy-start.1 = (f32[1152,512]{1,0:T(8,128)S(1)}, f32[1152,512]{1,0:T(8,128)}, u32[]{:S(2)}) copy-start(f32[1152,512]{1,0:T(8,128)} %param.16) | copy-start | bytes 7077892
  7.2 8.6 %copy-start.2 = (f32[1152,512]{1,0:T(8,128)S(1)}, f32[1152,512]{1,0:T(8,128)}, u32[]{:S(2)}) copy-start(f32[1152,512]{1,0:T(8,128)} %param.18) | copy-start | bytes 7077892
  7.2 8.6 %copy-start.3 = (f32[1152,512]{1,0:T(8,128)S(1)}, f32[1152,512]{1,0:T(8,128)}, u32[]{:S(2)}) copy-start(f32[1152,512]{1,0:T(8,128)} %param.17) | copy-start | bytes 7077892
  7.3 9.4 %copy-start.4 = (f32[1152,512]{1,0:T(8,128)S(1)}, f32[1152,512]{1,0:T(8,128)}, u32[]{:S(2)}) copy-start(f32[1152,512]{1,0:T(8,128)} %param.13) | copy-start | bytes 7077892
  7.3 10.2 %copy-start.5 = (f32[1152,512]{1,0:T(8,128)S(1)}, f32[1152,512]{1,0:T(8,128)}, u32[]{:S(2)}) copy-start(f32[1152,512]{1,0:T(8,128)} %param.15) | copy-start | bytes 7077892
  7.3 10.9 %copy-start.6 = (f32[1152,512]{1,0:T(8,128)S(1)}, f32[1152,512]{1,0:T(8,128)}, u32[]{:S(2)}) copy-start(f32[1152,512]{1,0:T(8,128)} %param.14) | copy-start | bytes 7077892
  34.3 3.1 copy-start.9
  34.3 3.1 copy-start.10
  34.3 4.5 %copy-start.8 = (f32[1024]{0:T(1024)}, f32[1024]{0:T(1024)S(1)}, u32[]{:S(2)}) copy-start(f32[1024]{0:T(1024)S(1)} %get-tuple-element.26) | copy-start | bytes 12292
  37.4 177.1 %all-gather.8.cloned.1.call-start = ((), (), s32[]{:S(2)}) async-start(), calls=%async_computation.2 | async-start | bytes 5898240 | tf_op jit(solution)/shard_map/all_gather | solution.py:47
  38.8 343.1 %all-gather.4.cloned.1.call-start = ((), (), s32[]{:S(2)}) async-start(), calls=%async_computation | async-start | bytes 11796480 | tf_op jit(solution)/shard_map/all_gather | solution.py:45
  390.4 5.0 %copy-start = (bf16[4608,512]{1,0:T(8,128)(2,1)S(1)}, bf16[4608,512]{1,0:T(8,128)(2,1)}, u32[]{:S(2)}) copy-start(bf16[4608,512]{1,0:T(8,128)(2,1)} %all-gather.8.cloned.1.call-done) | copy-start | bytes 14155780
Sparse Core Ops, SparseCore 0:
  37.5 87.5 all-gather.5
  126.7 87.7 all-gather.7
  216.7 165.1 all-gather.3
where the time goes:
time: 404 us
  waiting for transfers between devices  339 us (84%)
  other arithmetic  19.7 us (5%)
  local copies, waits for them, and re-layouts  18 us (4%)
  between operations  13.9 us (3%)
  blocking collectives  13.7 us (3%)
    all_gather x1, waiting for transfers between devices, body(): lax.all_gather(narrow_query, 'fsdp', axis=0, tiled=True)  167 us
    all_gather x1, waiting for transfers between devices, body(): lax.all_gather(narrow_value, 'fsdp', axis=0, tiled=True)  89.4 us
    all_gather x1, waiting for transfers between devices, body(): lax.all_gather(narrow_key, 'fsdp', axis=0, tiled=True)  81.8 us
    unnamed x25, local copies, waits for them, and re-layouts  18 us
    pmax x1, blocking collectives, body(): lax.pmax((jnp.max(jnp.abs(latest_gained_query), axis=0), jnp.max(jnp.abs(...  13.7 us
    reduce_max x1, other arithmetic, body(): jnp.max(jnp.abs(latest_gained_query), axis=0)  8.59 us
  transfers between devices with their start and end apart: 3, of which 3 were waited for; matrix products, arithmetic and copies ran while one was open for 1% of the time, Pallas kernels for 0%

commit v1 on v0

v1 whole, which is shorter than its diff:
```python
import functools

import jax
import jax.numpy as jnp
from jax import lax
from jax.experimental import pallas as pl
from jax.experimental.pallas import tpu as pltpu
from jax.sharding import PartitionSpec as P

learn_rate = 0.2
hold_rate = 0.8
AXIS = "fsdp"
MESH = pl.DeviceIdType.MESH
LANES = 128
AHEAD = 2
LAG = 2


def tile_of(rows, most=64):
    return max(t for t in range(16, most + 1, 16) if rows % t == 0)


def width_of(columns, most=256):
    return max(t for t in range(LANES, most + 1, LANES) if columns % t == 0)


def gather_kernel(n, chunks, *refs):
    params, gain_ref = refs[:9], refs[9]
    ready, scales = refs[10:13], refs[13:16]
    bufs = refs[16:19]
    gain_wide, mine, theirs = refs[19:22]
    load_sem, max_send, max_recv, send_sem, back_sem, recv_sem = refs[22:]
    rows = params[0].shape[0]
    tile = tile_of(rows)
    me = lax.axis_index(AXIS)

    def loads(c):
        a, offset, width = chunks[c]
        return [
            pltpu.make_async_copy(
                params[3 * a + k].at[:, pl.ds(offset, width)],
                bufs[a].at[k, :, pl.ds(offset, width)],
                load_sem.at[c, k],
            )
            for k in range(3)
        ]

    for c in range(min(AHEAD, len(chunks))):
        for copy in loads(c):
            copy.start()

    barrier = pltpu.get_barrier_semaphore()

    def greet(k, carry):
        pl.semaphore_signal(
            barrier, inc=1, device_id={AXIS: lax.rem(me + k, n)}, device_id_type=MESH
        )
        return carry

    lax.fori_loop(1, n, greet, 0)

    for k in range(gain_ref.shape[0]):
        block = jnp.broadcast_to(gain_ref[pl.ds(k, 1), :], (LANES, LANES))
        gain_wide[pl.ds(k * LANES, LANES), :] = block.T

    pl.semaphore_wait(barrier, n - 1)

    def max_copy(c, k):
        width = chunks[c][2] // LANES
        return pltpu.make_async_remote_copy(
            src_ref=mine.at[c, pl.ds(0, width)],
            dst_ref=theirs.at[c, k - 1, pl.ds(0, width)],
            send_sem=max_send.at[c, k - 1],
            recv_sem=max_recv.at[c, k - 1],
            device_id={AXIS: lax.rem(me + k, n)},
            device_id_type=MESH,
        )

    def step(c):
        a, offset, width = chunks[c]
        for copy in loads(c):
            copy.wait()
        parts = width // LANES

        def some(i, tops):
            r = pl.ds(pl.multiple_of(i * tile, tile), tile)
            gain = gain_wide[r, :]
            new = []
            for h in range(parts):
                cols = pl.ds(offset + h * LANES, LANES)
                hold = hold_rate * bufs[a][1, r, cols] + bufs[a][2, r, cols]
                gained = (bufs[a][0, r, cols] - learn_rate * hold) * gain
                bufs[a][0, r, cols] = gained
                top = jnp.max(jnp.abs(gained).reshape(tile // 8, 8, LANES), axis=0)
                new.append(jnp.maximum(tops[h], top))
            return tuple(new)

        tops = lax.fori_loop(
            0, rows // tile, some, tuple(jnp.zeros((8, LANES), jnp.float32) for _ in range(parts))
        )
        for h in range(parts):
            mine[c, h] = tops[h]

    def tell(c):
        def one(k, carry):
            max_copy(c, k).start()
            return carry

        lax.fori_loop(1, n, one, 0)

    def piece(c, block, target, sem):
        a, offset, width = chunks[c]
        where = ready[a].at[pl.ds(pl.multiple_of(block * rows, 16), rows), pl.ds(offset, width)]
        return pltpu.make_async_remote_copy(
            src_ref=where,
            dst_ref=where,
            send_sem=sem,
            recv_sem=recv_sem.at[block, c],
            device_id={AXIS: target},
            device_id_type=MESH,
        )

    def rightward(c, block):
        return piece(c, block, me + 1, send_sem.at[block, c])

    def leftward(c, block):
        return piece(c, block, me - 1, send_sem.at[block, c])

    def own_leftward(c):
        return piece(c, me, me - 1, back_sem.at[c])

    def finish(c):
        a, offset, width = chunks[c]

        def hear(k, carry):
            max_copy(c, k).wait_recv()
            return carry

        lax.fori_loop(1, n, hear, 0)
        parts = width // LANES
        tops = []
        for h in range(parts):
            top = lax.fori_loop(
                0, n - 1, lambda k, t: jnp.maximum(t, theirs[c, k, h]), mine[c, h]
            )
            top = jnp.max(top, axis=0, keepdims=True)
            scales[a][pl.ds(offset // LANES + h, 1), :] = top
            tops.append(top)

        def some(i, carry):
            r = pl.ds(pl.multiple_of(i * tile, tile), tile)
            to = pl.ds(pl.multiple_of(me * rows + i * tile, 16), tile)
            for h in range(parts):
                cols = pl.ds(offset + h * LANES, LANES)
                ready[a][to, cols] = (bufs[a][0, r, cols] / tops[h]).astype(jnp.bfloat16)
            return carry

        lax.fori_loop(0, rows // tile, some, 0)

        @pl.when(me < n - 1)
        def _():
            rightward(c, me).start()

        @pl.when(me > 0)
        def _():
            own_leftward(c).start()

    total = len(chunks)
    for c in range(total + LAG):
        if c < total:
            step(c)
            if c + AHEAD < total:
                for copy in loads(c + AHEAD):
                    copy.start()
            tell(c)
        if c >= LAG:
            finish(c - LAG)

    def hop(s, carry):
        for c in range(total):

            @pl.when(me - s >= 0)
            def _():
                block = me - s
                rightward(c, block).wait_recv()

                @pl.when(me < n - 1)
                def _():
                    rightward(c, block).start()

            @pl.when(me + s < n)
            def _():
                block = me + s
                leftward(c, block).wait_recv()

                @pl.when(me > 0)
                def _():
                    leftward(c, block).start()

        return carry

    lax.fori_loop(1, n, hop, 0)

    def close(s, carry):
        for c in range(total):

            @pl.when((me - s >= 0) & (me < n - 1))
            def _():
                rightward(c, me - s).wait_send()

            @pl.when((me + s < n) & (me > 0) & (s > 0))
            def _():
                leftward(c, me + s).wait_send()

        return carry

    lax.fori_loop(0, n, close, 0)
    for c in range(total):

        @pl.when(me > 0)
        def _():
            own_leftward(c).wait_send()

        def sent(k, carry):
            max_copy(c, k).wait_send()
            return carry

        lax.fori_loop(1, n, sent, 0)


def store_kernel(cuts, *refs):
    sources, targets, sem = refs[:6], refs[6:12], refs[12]
    copies = []
    for a in range(6):
        pieces = cuts if a < 3 else 1
        height = sources[a].shape[0] // pieces
        for k in range(pieces):
            part = pl.ds(k * height, height)
            copies.append(
                pltpu.make_async_copy(sources[a].at[part], targets[a].at[part], sem.at[a, k])
            )
    for copy in copies:
        copy.start()
    for copy in copies:
        copy.wait()


def body(n, *args):
    params, gain = args[:9], args[9]
    rows = params[0].shape[0]
    widths = [params[3 * a].shape[1] for a in range(3)]
    chunks = []
    for a in (1, 2, 0):
        width = width_of(widths[a])
        chunks += [(a, offset, width) for offset in range(0, widths[a], width)]
    total = len(chunks)
    wide = max(width for _, _, width in chunks) // LANES
    groups = -(-rows // LANES)
    if groups * LANES != rows:
        gain = jnp.pad(gain, (0, groups * LANES - rows))
    gain = gain.reshape(groups, LANES)
    shapes = [((n * rows, width), jnp.bfloat16) for width in widths]
    shapes += [((width // LANES, LANES), jnp.float32) for width in widths]
    gathered = pl.pallas_call(
        functools.partial(gather_kernel, n, tuple(chunks)),
        out_shape=[pltpu.VMEM(shape, dtype) for shape, dtype in shapes],
        in_specs=[pl.BlockSpec(memory_space=pl.ANY)] * 9 + [pl.BlockSpec(memory_space=pltpu.VMEM)],
        out_specs=[pl.BlockSpec(memory_space=pltpu.VMEM)] * 6,
        scratch_shapes=[pltpu.VMEM((3, rows, width), jnp.float32) for width in widths]
        + [
            pltpu.VMEM((groups * LANES, LANES), jnp.float32),
            pltpu.VMEM((total, wide, 8, LANES), jnp.float32),
            pltpu.VMEM((total, n - 1, wide, 8, LANES), jnp.float32),
            pltpu.SemaphoreType.DMA((total, 3)),
            pltpu.SemaphoreType.DMA((total, n - 1)),
            pltpu.SemaphoreType.DMA((total, n - 1)),
            pltpu.SemaphoreType.DMA((n, total)),
            pltpu.SemaphoreType.DMA((total,)),
            pltpu.SemaphoreType.DMA((n, total)),
        ],
        compiler_params=pltpu.CompilerParams(
            collective_id=0, has_side_effects=True, vmem_limit_bytes=40 * 2**20
        ),
        name="gather",
    )(*params, gain)
    cuts = 4
    stored = pl.pallas_call(
        functools.partial(store_kernel, cuts),
        out_shape=[jax.ShapeDtypeStruct(shape, dtype) for shape, dtype in shapes],
        in_specs=[pl.BlockSpec(memory_space=pltpu.VMEM)] * 6,
        out_specs=[pl.BlockSpec(memory_space=pl.ANY)] * 6,
        scratch_shapes=[pltpu.SemaphoreType.DMA((6, cuts))],
        compiler_params=pltpu.CompilerParams(vmem_limit_bytes=2**20),
        name="store",
    )(*gathered)
    return (*stored[:3], *(s.reshape(-1) for s in stored[3:]))


def solution(mesh):
    matrix = P(("shift", AXIS), "model")
    column = P(("shift", "model"))
    whole = P("shift", "model")
    return jax.shard_map(
        functools.partial(body, mesh.shape[AXIS]),
        mesh=mesh,
        in_specs=(matrix,) * 9 + (P(("shift", AXIS)),),
        out_specs=(whole, whole, whole, column, column, column),
        check_vma=False,
    )
```

time: 404 us -> 326 us (0.81)
  waiting for transfers between devices: 339 us -> 0 us
  Pallas kernels: 0 us -> 325 us
  other arithmetic: 19.7 us -> 0 us
  local copies, waits for them, and re-layouts: 18 us -> 0 us
  blocking collectives: 13.7 us -> 0 us
  between operations: 13.9 us -> 0.64 us
    all_gather x3 -> x0, waiting for transfers between devices: 339 us -> none  [the longest x1 167 us: body(): lax.all_gather(narrow_query, 'fsdp', axis=0, tiled=True)]
    pallas_call x0 -> x2, Pallas kernels: none -> 325 us  [the longest x1 318 us: body(): pl.pallas_call(functools.partial(gather_kernel, n, tuple(chunks)), out_sh...]
    unnamed x25 -> x0, local copies, waits for them, and re-layouts: 18 us -> none
    pmax x1 -> x0, blocking collectives: 13.7 us -> none  [body(): lax.pmax((jnp.max(jnp.abs(latest_gained_query), axis=0), jnp.max(jnp.abs(...]
    reduce_max x2 -> x0, other arithmetic: 11 us -> none  [the longest x1 8.59 us: body(): jnp.max(jnp.abs(latest_gained_query), axis=0)]
    convert_element_type x3 -> x0, other arithmetic: 8.74 us -> none  [the longest x1 4.42 us: body(): (latest_gained_query / scale_query).astype(jnp.bfloat16)]
  transfers between devices with their start and end apart: 3 -> 0, of which waited for: 3 -> 0; matrix products, arithmetic and copies ran while one was open for 1% -> 0% of each run, Pallas kernels for 0% -> 0%
where the time goes in v1:
time: 326 us
  Pallas kernels  325 us (100%)
    pallas_call x1, Pallas kernels, body(): pl.pallas_call(functools.partial(gather_kernel, n, tuple(chunks)), out_sh...  318 us
    pallas_call x1, Pallas kernels, body(): pl.pallas_call(functools.partial(store_kernel, cuts), out_shape=[jax.Shap...  6.69 us

profile of v1, /device:TPU:0, one launch (start us, length us, event | category | flops | bytes accessed | tf_op | source)
XLA Modules:
  0.0 325.8 jit_solution(1588595123884844173)
XLA Ops:
  0.6 318.5 %gather.1 = (bf16[4608,1024]{1,0:T(8,128)(2,1)S(1)}, bf16[4608,512]{1,0:T(8,128)(2,1)S(1)}, bf16[4608,512]{1,0:T(8,128)(2,1)S(1)}, f32[8,128]{1,0:T(8,128)S(1)},...) custom-call(f32[1152,1024]{1,0:T(8,128)} %refs_0_.1, f32[1152,1024]{1,0:T(8,128)} %refs_1_.1, f32[1152,1024]{1,0:T(8,128)} %refs_2_.1, ...), custom_call_target="tpu_custom_call" | custom-call | tf_op jit(solution)/shard_map/gather/pallas_call | solution.py:264
  319.1 6.7 %store.1 = (bf16[4608,1024]{1,0:T(8,128)(2,1)}, bf16[4608,512]{1,0:T(8,128)(2,1)}, bf16[4608,512]{1,0:T(8,128)(2,1)}, f32[8,128]{1,0:T(8,128)}, f32[4,128]{1,0:T(4,128)}, /*index=5*/f32[4,128]{1,0:T(4,128)}) custom-call(bf16[4608,1024]{1,0:T(8,128)(2,1)S(1)} %get-tuple-element.18.refs_0_, bf16[4608,512]{1,0:T(8,128)(2,1)S(1)} %get-tuple-element.19.refs_1_, ...), custom_call_target="tpu_custom_call" | custom-call | tf_op jit(solution)/shard_map/store/pallas_call | solution.py:287

commit v2 on v1

--- a/solution.py
+++ b/solution.py
@@ -26,10 +26,11 @@
 
 def gather_kernel(n, chunks, *refs):
     params, gain_ref = refs[:9], refs[9]
-    ready, scales = refs[10:13], refs[13:16]
-    bufs = refs[16:19]
-    gain_wide, mine, theirs = refs[19:22]
-    load_sem, max_send, max_recv, send_sem, back_sem, recv_sem = refs[22:]
+    ready, scales, last = refs[10:13], refs[13:16], refs[16]
+    bufs = refs[17:20]
+    gain_wide, mine, theirs = refs[20:23]
+    load_sem, max_send, max_recv, send_sem, back_sem, recv_sem, last_sem = refs[23:]
+    total = len(chunks)
     rows = params[0].shape[0]
     tile = tile_of(rows)
     me = lax.axis_index(AXIS)
@@ -45,9 +46,8 @@
             for k in range(3)
         ]
 
-    for c in range(min(AHEAD, len(chunks))):
-        for copy in loads(c):
-            copy.start()
+    for copy in loads(0):
+        copy.start()
 
     barrier = pltpu.get_barrier_semaphore()
 
@@ -59,11 +59,13 @@
 
     lax.fori_loop(1, n, greet, 0)
 
+    for c in range(1, min(AHEAD, len(chunks))):
+        for copy in loads(c):
+            copy.start()
+
     for k in range(gain_ref.shape[0]):
         block = jnp.broadcast_to(gain_ref[pl.ds(k, 1), :], (LANES, LANES))
         gain_wide[pl.ds(k * LANES, LANES), :] = block.T
-
-    pl.semaphore_wait(barrier, n - 1)
 
     def max_copy(c, k):
         width = chunks[c][2] // LANES
@@ -129,6 +131,17 @@
     def own_leftward(c):
         return piece(c, me, me - 1, back_sem.at[c])
 
+    def goes_right(c):
+        return (me < n - 2) if c == total - 1 else (me < n - 1)
+
+    def goes_left(c):
+        return (me > 1) if c == total - 1 else (me > 0)
+
+    def keep():
+        a, offset, width = chunks[-1]
+        own = ready[a].at[pl.ds(pl.multiple_of(me * rows, 16), rows), pl.ds(offset, width)]
+        return pltpu.make_async_copy(own, last, last_sem)
+
     def finish(c):
         a, offset, width = chunks[c]
 
@@ -157,21 +170,25 @@
 
         lax.fori_loop(0, rows // tile, some, 0)
 
-        @pl.when(me < n - 1)
+        if c == total - 1:
+            keep().start()
+
+        @pl.when(goes_right(c))
         def _():
             rightward(c, me).start()
 
-        @pl.when(me > 0)
+        @pl.when(goes_left(c))
         def _():
             own_leftward(c).start()
 
-    total = len(chunks)
     for c in range(total + LAG):
         if c < total:
             step(c)
             if c + AHEAD < total:
                 for copy in loads(c + AHEAD):
                     copy.start()
+            if c == 0:
+                pl.semaphore_wait(barrier, n - 1)
             tell(c)
         if c >= LAG:
             finish(c - LAG)
@@ -179,7 +196,12 @@
     def hop(s, carry):
         for c in range(total):
 
-            @pl.when(me - s >= 0)
+            from_left, from_right = me - s >= 0, me + s < n
+            if c == total - 1:
+                from_left &= (me < n - 1) | (s > 1)
+                from_right &= (me > 0) | (s > 1)
+
+            @pl.when(from_left)
             def _():
                 block = me - s
                 rightward(c, block).wait_recv()
@@ -188,7 +210,7 @@
                 def _():
                     rightward(c, block).start()
 
-            @pl.when(me + s < n)
+            @pl.when(from_right)
             def _():
                 block = me + s
                 leftward(c, block).wait_recv()
@@ -204,7 +226,11 @@
     def close(s, carry):
         for c in range(total):
 
-            @pl.when((me - s >= 0) & (me < n - 1))
+            to_right = (me - s >= 0) & (me < n - 1)
+            if c == total - 1:
+                to_right &= (me < n - 2) | (s > 0)
+
+            @pl.when(to_right)
             def _():
                 rightward(c, me - s).wait_send()
 
@@ -215,9 +241,10 @@
         return carry
 
     lax.fori_loop(0, n, close, 0)
+    keep().wait()
     for c in range(total):
 
-        @pl.when(me > 0)
+        @pl.when(goes_left(c))
         def _():
             own_leftward(c).wait_send()
 
@@ -245,6 +272,23 @@
         copy.wait()
 
 
+def patch_kernel(n, offset, old_ref, piece_ref, new_ref, sem):
+    del old_ref
+    rows, width = piece_ref.shape
+    me = lax.axis_index(AXIS)
+
+    @pl.when((me == 0) | (me == n - 1))
+    def _():
+        block = jnp.where(me == 0, 1, n - 2)
+        copy = pltpu.make_async_copy(
+            piece_ref,
+            new_ref.at[pl.ds(pl.multiple_of(block * rows, 16), rows), pl.ds(offset, width)],
+            sem,
+        )
+        copy.start()
+        copy.wait()
+
+
 def body(n, *args):
     params, gain = args[:9], args[9]
     rows = params[0].shape[0]
@@ -253,7 +297,12 @@
     for a in (1, 2, 0):
         width = width_of(widths[a])
         chunks += [(a, offset, width) for offset in range(0, widths[a], width)]
+    a, offset, width = chunks[0]
+    chunks[:1] = [(a, offset + part, LANES) for part in range(0, width, LANES)]
+    a, offset, width = chunks[-1]
+    chunks[-1:] = [(a, offset + part, LANES) for part in range(0, width, LANES)]
     total = len(chunks)
+    last_array, last_offset, last_width = chunks[-1]
     wide = max(width for _, _, width in chunks) // LANES
     groups = -(-rows // LANES)
     if groups * LANES != rows:
@@ -263,9 +312,10 @@
     shapes += [((width // LANES, LANES), jnp.float32) for width in widths]
     gathered = pl.pallas_call(
         functools.partial(gather_kernel, n, tuple(chunks)),
-        out_shape=[pltpu.VMEM(shape, dtype) for shape, dtype in shapes],
+        out_shape=[pltpu.VMEM(shape, dtype) for shape, dtype in shapes]
+        + [jax.ShapeDtypeStruct((rows, last_width), jnp.bfloat16)],
         in_specs=[pl.BlockSpec(memory_space=pl.ANY)] * 9 + [pl.BlockSpec(memory_space=pltpu.VMEM)],
-        out_specs=[pl.BlockSpec(memory_space=pltpu.VMEM)] * 6,
+        out_specs=[pl.BlockSpec(memory_space=pltpu.VMEM)] * 6 + [pl.BlockSpec(memory_space=pl.ANY)],
         scratch_shapes=[pltpu.VMEM((3, rows, width), jnp.float32) for width in widths]
         + [
             pltpu.VMEM((groups * LANES, LANES), jnp.float32),
@@ -277,12 +327,15 @@
             pltpu.SemaphoreType.DMA((n, total)),
             pltpu.SemaphoreType.DMA((total,)),
             pltpu.SemaphoreType.DMA((n, total)),
+            pltpu.SemaphoreType.DMA,
         ],
         compiler_params=pltpu.CompilerParams(
             collective_id=0, has_side_effects=True, vmem_limit_bytes=40 * 2**20
         ),
         name="gather",
     )(*params, gain)
+    *gathered, last = gathered
+    piece = lax.ppermute(last, AXIS, ((n - 2, n - 1), (1, 0)))
     cuts = 4
     stored = pl.pallas_call(
         functools.partial(store_kernel, cuts),
@@ -291,8 +344,21 @@
         out_specs=[pl.BlockSpec(memory_space=pl.ANY)] * 6,
         scratch_shapes=[pltpu.SemaphoreType.DMA((6, cuts))],
         compiler_params=pltpu.CompilerParams(vmem_limit_bytes=2**20),
+        cost_estimate=pl.CostEstimate(flops=0, bytes_accessed=4 * n * rows * sum(widths), transcendentals=0),
         name="store",
     )(*gathered)
+    stored = list(stored)
+    shape, dtype = shapes[last_array]
+    stored[last_array] = pl.pallas_call(
+        functools.partial(patch_kernel, n, last_offset),
+        out_shape=jax.ShapeDtypeStruct(shape, dtype),
+        in_specs=[pl.BlockSpec(memory_space=pl.ANY), pl.BlockSpec(memory_space=pltpu.VMEM)],
+        out_specs=pl.BlockSpec(memory_space=pl.ANY),
+        scratch_shapes=[pltpu.SemaphoreType.DMA],
+        input_output_aliases={0: 0},
+        compiler_params=pltpu.CompilerParams(vmem_limit_bytes=2**20),
+        name="patch",
+    )(stored[last_array], piece)
     return (*stored[:3], *(s.reshape(-1) for s in stored[3:]))
 
 

time: 326 us -> 324 us (level)
  Pallas kernels: 325 us -> 320 us
    pallas_call x1, Pallas kernels: 318 us -> 312 us  [body(): pl.pallas_call(functools.partial(gather_kernel, n, tuple(chunks)), out_sh...]
  transfers between devices with their start and end apart: 0 -> 1, of which waited for: 0 -> 1; matrix products, arithmetic and copies ran while one was open for 0% -> 0% of each run, Pallas kernels for 0% -> 2%
where the time goes in v2:
time: 324 us; the launch traced here: 323 us
  Pallas kernels  320 us (99%)
    pallas_call x1, Pallas kernels, body(): pl.pallas_call(functools.partial(gather_kernel, n, tuple(chunks)), out_sh...  312 us
    pallas_call x1, Pallas kernels, body(): pl.pallas_call(functools.partial(store_kernel, cuts), out_shape=[jax.Shap...  6.69 us
  transfers between devices with their start and end apart: 1, of which 1 were waited for; matrix products, arithmetic and copies ran while one was open for 0% of the time, Pallas kernels for 2%

profile of v2, /device:TPU:0, one launch (start us, length us, event | category | flops | bytes accessed | tf_op | source)
XLA Modules:
  0.0 323.3 jit_solution(12752837507690189148)
XLA Ops:
  0.6 312.3 %gather.1 = (bf16[4608,1024]{1,0:T(8,128)(2,1)S(1)}, bf16[4608,512]{1,0:T(8,128)(2,1)S(1)}, bf16[4608,512]{1,0:T(8,128)(2,1)S(1)}, f32[8,128]{1,0:T(8,128)S(1)},...) custom-call(f32[1152,1024]{1,0:T(8,128)} %refs_0_.1, f32[1152,1024]{1,0:T(8,128)} %refs_1_.1, ...), custom_call_target="tpu_custom_call" | custom-call | tf_op jit(solution)/shard_map/gather/pallas_call | solution.py:313
  312.9 1.3 collective-permute-start
  314.2 6.7 %store.1 = (bf16[4608,1024]{1,0:T(8,128)(2,1)}, bf16[4608,512]{1,0:T(8,128)(2,1)}, bf16[4608,512]{1,0:T(8,128)(2,1)}, f32[8,128]{1,0:T(8,128)}, f32[4,128]{1,0:T(4,128)}, /*index=5*/f32[4,128]{1,0:T(4,128)}) custom-call(bf16[4608,1024]{1,0:T(8,128)(2,1)S(1)} %get-tuple-element.19.refs_0_, bf16[4608,512]{1,0:T(8,128)(2,1)S(1)} %get-tuple-element.20.refs_1_, ...), custom_call_target="tpu_custom_call" | custom-call | bytes 37748736 | tf_op jit(solution)/shard_map/store/pallas_call | solution.py:340
  320.9 1.6 collective-permute-done.piece_ref
  322.5 0.7 patch.1
Async XLA Ops:
  312.9 9.6 %collective-permute-start = (bf16[1152,128]{1,0:T(8,128)(2,1)}, bf16[1152,128]{1,0:T(8,128)(2,1)S(1)}, u32[]{:S(2)}, u32[]{:S(2)}) collective-permute-start(bf16[1152,128]{1,0:T(8,128)(2,1)} %get-tuple-element.26), channel_id=1, source_target_pairs={{16,24},{8,0},{17,25},{9,1},{18,26},{10,2},{19,27},{11,3},{20,28},... | collective-permute-start | bytes 884744 | tf_op jit(solution)/shard_map/ppermute | solution.py:338

commit v3 on v2

--- a/solution.py
+++ b/solution.py
@@ -13,7 +13,7 @@
 MESH = pl.DeviceIdType.MESH
 LANES = 128
 AHEAD = 2
-LAG = 2
+LAG = 1
 
 
 def tile_of(rows, most=64):
@@ -25,11 +25,11 @@
 
 
 def gather_kernel(n, chunks, *refs):
-    params, gain_ref = refs[:9], refs[9]
+    params, gain_hbm = refs[:9], refs[9]
     ready, scales, last = refs[10:13], refs[13:16], refs[16]
     bufs = refs[17:20]
     gain_wide, mine, theirs = refs[20:23]
-    load_sem, max_send, max_recv, send_sem, back_sem, recv_sem, last_sem = refs[23:]
+    load_sem, max_send, max_recv, send_sem, back_sem, recv_sem, last_sem, gain_ref, gain_sem = refs[23:]
     total = len(chunks)
     rows = params[0].shape[0]
     tile = tile_of(rows)
@@ -46,6 +46,8 @@
             for k in range(3)
         ]
 
+    gain_load = pltpu.make_async_copy(gain_hbm, gain_ref, gain_sem)
+    gain_load.start()
     for copy in loads(0):
         copy.start()
 
@@ -59,13 +61,14 @@
 
     lax.fori_loop(1, n, greet, 0)
 
-    for c in range(1, min(AHEAD, len(chunks))):
-        for copy in loads(c):
-            copy.start()
-
+    gain_load.wait()
     for k in range(gain_ref.shape[0]):
         block = jnp.broadcast_to(gain_ref[pl.ds(k, 1), :], (LANES, LANES))
         gain_wide[pl.ds(k * LANES, LANES), :] = block.T
+
+    for c in range(1, min(AHEAD, total)):
+        for copy in loads(c):
+            copy.start()
 
     def max_copy(c, k):
         width = chunks[c][2] // LANES
@@ -193,9 +196,31 @@
         if c >= LAG:
             finish(c - LAG)
 
+    def sent(c, s):
+        to_right = (me - s >= 0) & (me < n - 1)
+        to_left = (me + s < n) & (me > 0) & (s > 0)
+        if c == total - 1:
+            to_right &= (me < n - 2) | (s > 0)
+
+        @pl.when(to_right)
+        def _():
+            rightward(c, me - s).wait_send()
+
+        @pl.when(to_left)
+        def _():
+            leftward(c, me + s).wait_send()
+
+    for c in range(total):
+
+        def told(k, carry):
+            max_copy(c, k).wait_send()
+            return carry
+
+        lax.fori_loop(1, n, told, 0)
+    keep().wait()
+
     def hop(s, carry):
         for c in range(total):
-
             from_left, from_right = me - s >= 0, me + s < n
             if c == total - 1:
                 from_left &= (me < n - 1) | (s > 1)
@@ -219,40 +244,17 @@
                 def _():
                     leftward(c, block).start()
 
+            sent(c, s - 1)
+
+            @pl.when(goes_left(c) & (s == 1))
+            def _():
+                own_leftward(c).wait_send()
+
         return carry
 
     lax.fori_loop(1, n, hop, 0)
-
-    def close(s, carry):
-        for c in range(total):
-
-            to_right = (me - s >= 0) & (me < n - 1)
-            if c == total - 1:
-                to_right &= (me < n - 2) | (s > 0)
-
-            @pl.when(to_right)
-            def _():
-                rightward(c, me - s).wait_send()
-
-            @pl.when((me + s < n) & (me > 0) & (s > 0))
-            def _():
-                leftward(c, me + s).wait_send()
-
-        return carry
-
-    lax.fori_loop(0, n, close, 0)
-    keep().wait()
     for c in range(total):
-
-        @pl.when(goes_left(c))
-        def _():
-            own_leftward(c).wait_send()
-
-        def sent(k, carry):
-            max_copy(c, k).wait_send()
-            return carry
-
-        lax.fori_loop(1, n, sent, 0)
+        sent(c, n - 1)
 
 
 def store_kernel(cuts, *refs):
@@ -314,7 +316,7 @@
         functools.partial(gather_kernel, n, tuple(chunks)),
         out_shape=[pltpu.VMEM(shape, dtype) for shape, dtype in shapes]
         + [jax.ShapeDtypeStruct((rows, last_width), jnp.bfloat16)],
-        in_specs=[pl.BlockSpec(memory_space=pl.ANY)] * 9 + [pl.BlockSpec(memory_space=pltpu.VMEM)],
+        in_specs=[pl.BlockSpec(memory_space=pl.ANY)] * 10,
         out_specs=[pl.BlockSpec(memory_space=pltpu.VMEM)] * 6 + [pl.BlockSpec(memory_space=pl.ANY)],
         scratch_shapes=[pltpu.VMEM((3, rows, width), jnp.float32) for width in widths]
         + [
@@ -327,6 +329,8 @@
             pltpu.SemaphoreType.DMA((n, total)),
             pltpu.SemaphoreType.DMA((total,)),
             pltpu.SemaphoreType.DMA((n, total)),
+            pltpu.SemaphoreType.DMA,
+            pltpu.VMEM((groups, LANES), jnp.float32),
             pltpu.SemaphoreType.DMA,
         ],
         compiler_params=pltpu.CompilerParams(

time: 324 us -> 323 us (level)
  no operation moved by 1% of the time
where the time goes in v3:
time: 323 us; the launch traced here: 322 us
  Pallas kernels  319 us (99%)
    pallas_call x1, Pallas kernels, body(): pl.pallas_call(functools.partial(gather_kernel, n, tuple(chunks)), out_sh...  312 us
    pallas_call x1, Pallas kernels, body(): pl.pallas_call(functools.partial(store_kernel, cuts), out_shape=[jax.Shap...  6.69 us
  transfers between devices with their start and end apart: 1, of which 1 were waited for; matrix products, arithmetic and copies ran while one was open for 0% of the time, Pallas kernels for 2%

profile of v3, /device:TPU:0, one launch (start us, length us, event | category | flops | bytes accessed | tf_op | source)
XLA Modules:
  0.0 322.4 jit_solution(10191321343488583732)
XLA Ops:
  0.6 311.6 %gather.1 = (bf16[4608,1024]{1,0:T(8,128)(2,1)S(1)}, bf16[4608,512]{1,0:T(8,128)(2,1)S(1)}, bf16[4608,512]{1,0:T(8,128)(2,1)S(1)}, f32[8,128]{1,0:T(8,128)S(1)},...) custom-call(f32[1152,1024]{1,0:T(8,128)} %refs_0_.1, f32[1152,1024]{1,0:T(8,128)} %refs_1_.1, ...), custom_call_target="tpu_custom_call" | custom-call | tf_op jit(solution)/shard_map/gather/pallas_call | solution.py:315
  312.2 1.3 collective-permute-start
  313.5 6.7 %store.1 = (bf16[4608,1024]{1,0:T(8,128)(2,1)}, bf16[4608,512]{1,0:T(8,128)(2,1)}, bf16[4608,512]{1,0:T(8,128)(2,1)}, f32[8,128]{1,0:T(8,128)}, f32[4,128]{1,0:T(4,128)}, /*index=5*/f32[4,128]{1,0:T(4,128)}) custom-call(bf16[4608,1024]{1,0:T(8,128)(2,1)S(1)} %get-tuple-element.19.refs_0_, bf16[4608,512]{1,0:T(8,128)(2,1)S(1)} %get-tuple-element.20.refs_1_, ...), custom_call_target="tpu_custom_call" | custom-call | bytes 37748736 | tf_op jit(solution)/shard_map/store/pallas_call | solution.py:344
  320.2 1.4 collective-permute-done.piece_ref
  321.6 0.7 patch.1
Async XLA Ops:
  312.2 9.4 %collective-permute-start = (bf16[1152,128]{1,0:T(8,128)(2,1)}, bf16[1152,128]{1,0:T(8,128)(2,1)S(1)}, u32[]{:S(2)}, u32[]{:S(2)}) collective-permute-start(bf16[1152,128]{1,0:T(8,128)(2,1)} %get-tuple-element.26), channel_id=1, source_target_pairs={{16,24},{8,0},{17,25},{9,1},{18,26},{10,2},{19,27},{11,3},{20,28},... | collective-permute-start | bytes 884744 | tf_op jit(solution)/shard_map/ppermute | solution.py:342
